TPU v7x, 256 devices: a whole 4x4x8 slice. The times are simulated.
256 devices in a mesh: ens: 4 (over z_lo, core), gx: 16 (over x, z_hi), gy: 4 (over y).
Axes of the slice: x: 4, y: 4, z: 8 (z_hi: 4, z_lo: 2; z = z_hi * 2 + z_lo), core: 2. Of those that a mesh axis runs over, the one named last changes fastest.
Arguments:
- members: bfloat16 [64, 75, 256, 512], P(('ens', 'gx'), None, None, 'gy'), may hold values from -0.75 to 0.75
- spread: bfloat16 [75, 75], replicated, as said below
- sea_mask: int32 [256, 512], P(('ens', 'gx'), 'gy'), may hold values 0 or 1
- innovations: float32 [75, 256, 512], P(None, ('ens', 'gx'), 'gy'), may hold values from -19 to 19
- obs_error: float32 [75, 256, 512], P(None, ('ens', 'gx'), 'gy'), may hold values from 0.3 to 3
- static_scale: float32 [75, 256, 512], P(None, ('ens', 'gx'), 'gy'), may hold values from 2 to 8
Outputs:
- increment: float32 [75, 256, 512], P(None, ('ens', 'gx'), 'gy')
- alpha_fields: bfloat16 [64, 75, 256, 512], P(('ens', 'gx'), None, None, 'gy')
Inputs may be any that keep to these rules, and one draw needn't show every extreme that they name: `spread`: symmetric and positive definite. `sea_mask`: 1 marks sea, 0 land.
All inputs are finite; a program needn't handle non-finite values. No bound on the sum of `sea_mask` on one device may be relied on, other than what follows from the above.
Results may differ from a plain program's by a relative error of at most 0.0065.
Values may be sent and summed in bfloat16 or wider, within the bound.
No kernel may reach another device: no remote copies, remote signals or barrier semaphores. Data moves between devices by JAX's collectives and lax.ppermute only.
A program may use at most 128 MiB of HBM per device.

v0:
```python
import jax
import jax.numpy as jnp
from jax import lax
from jax.sharding import Mesh
from jax.sharding import PartitionSpec as P

GRIDS = 3
SWEEPS = 2
COARSE_SWEEPS = 4
ITERATIONS = 3
ENS_GX_GY = ("ens_0", "ens_1", "gx_0", "gx_1", "gy")
ENS_GX = ("ens_0", "ens_1", "gx_0", "gx_1")
diffusivity = 16.0
damping = 0.8


def padded_2(x, sides, width):
    edges = {}
    for axis, dim in sides:
        size, length = (lax.axis_size(axis), x.shape[dim])
        up = [(i, (i + 1) % size) for i in range(size - 1)]
        last = lax.slice_in_dim(x, length - width, length, axis=dim)
        leading = lax.slice_in_dim(x, 0, width, axis=dim)
        edges[dim] = (
            lax.ppermute(last, axis, up),
            lax.ppermute(leading, axis, [(b, a) for a, b in up]),
        )
    done = []
    for _, dim in sides:
        low, high = edges[dim]
        around = [(width, width) if d in done else (0, 0) for d in range(x.ndim)]
        x = jnp.concatenate([jnp.pad(low, around), x, jnp.pad(high, around)], axis=dim)
        done.append(dim)
    return x


def by_axis(x, axes):
    for axis in axes:
        x = lax.psum(x, axis)
    return x


def neighbours(padded):
    return padded[:, 2:, 1:-1] + padded[:, :-2, 1:-1] + padded[:, 1:-1, 2:] + padded[:, 1:-1, :-2]


def apply_level(values, strength, padded):
    return values + strength * (4.0 * values - neighbours(padded))


def relax(values, source, strength, padded):
    return values + damping * (source - apply_level(values, strength, padded)) / (
        1.0 + 4.0 * strength
    )


def framed(values):
    return padded_2(values.astype(jnp.bfloat16), ((ENS_GX, 1), ("gy", 2)), 1).astype(values.dtype)


def restrict(values):
    layer_count, row_count, column_count = values.shape
    return 0.25 * values.reshape(layer_count, row_count // 2, 2, column_count // 2, 2).sum(
        axis=(2, 4)
    )


def prolong(values):
    layer_count, row_count, column_count = values.shape
    spread_out = jnp.broadcast_to(
        values[:, :, None, :, None], (layer_count, row_count, 2, column_count, 2)
    )
    return spread_out.reshape(layer_count, 2 * row_count, 2 * column_count)


def coarse_solve(source, strength):
    factor = damping / (1.0 + 4.0 * strength)
    solution = factor * source
    for sweep_index in range(COARSE_SWEEPS - 1):
        padded = padded_2(solution, ((ENS_GX, 1), ("gy", 2)), 1)
        solution = relax(solution, source, strength, padded)
    return solution


def vcycle(source, grid_level):
    strength = diffusivity / 4.0**grid_level
    if grid_level == GRIDS - 1:
        return coarse_solve(source, strength)
    solution = damping / (1.0 + 4.0 * strength) * source
    solution = relax(solution, source, strength, framed(solution))
    remainder = source - apply_level(solution, strength, framed(solution))
    solution = solution + prolong(vcycle(restrict(remainder), grid_level + 1))
    for sweep_index in range(SWEEPS):
        solution = relax(solution, source, strength, framed(solution))
    return solution


def member_products(tiles, spread, masked):
    member_count, layer_count, row_count, column_count = tiles.shape
    product = (tiles * masked).astype(jnp.bfloat16)
    flat = product.reshape(member_count, layer_count, row_count * column_count)
    mixed = jnp.einsum("ij,kjc->kic", spread, flat, preferred_element_type=jnp.float32)
    return mixed.reshape(tiles.shape)


def local(members, spread, sea_mask, innovations, obs_error, static_scale):
    tiles = lax.all_to_all(members, ENS_GX, split_axis=2, concat_axis=0, tiled=True)
    sea = sea_mask.astype(jnp.float32)[None]

    def covariance(direction):
        masked = sea * direction
        mixed = member_products(tiles, spread, masked)
        ensemble = jnp.sum(tiles * mixed, axis=0)
        static = static_scale * vcycle(static_scale * masked, 0)
        return sea * (ensemble + static)

    def system(direction):
        cov_dir = covariance(direction)
        return (cov_dir, cov_dir + obs_error * direction)

    def merged(residual, image):
        return (
            by_axis(jnp.sum(residual * residual), ENS_GX_GY),
            by_axis(jnp.sum(residual * image), ENS_GX_GY),
        )

    weights = jnp.zeros_like(innovations)
    increment = jnp.zeros_like(innovations)
    residual = innovations
    cov_res, image_res = system(residual)
    norm_now, product = merged(residual, image_res)
    alpha = norm_now / product
    direction, along, cov_dir = (residual, image_res, cov_res)
    for iteration in range(ITERATIONS):
        weights = weights + alpha * direction
        increment = increment + alpha * cov_dir
        residual = residual - alpha * along
        if iteration + 1 < ITERATIONS:
            cov_res, image_res = system(residual)
            norm_next, product = merged(residual, image_res)
            ratio = norm_next / norm_now
            alpha = norm_next / (product - ratio * norm_next / alpha)
            direction = residual + ratio * direction
            along = image_res + ratio * along
            cov_dir = cov_res + ratio * cov_dir
            norm_now = norm_next
    final = member_products(tiles, spread, sea * weights).astype(jnp.bfloat16)
    alpha_fields = lax.all_to_all(final, ENS_GX, split_axis=0, concat_axis=2, tiled=True)
    return (increment, alpha_fields)


def solution(mesh):
    split = Mesh(
        mesh.devices.reshape(2, 2, 4, 4, mesh.shape["gy"]), ("ens_0", "ens_1", "gx_0", "gx_1", "gy")
    )
    return jax.shard_map(
        local,
        mesh=split,
        in_specs=(
            P(ENS_GX, None, None, "gy"),
            P(),
            P(ENS_GX, "gy"),
            P(None, ENS_GX, "gy"),
            P(None, ENS_GX, "gy"),
            P(None, ENS_GX, "gy"),
        ),
        out_specs=(P(None, ENS_GX, "gy"), P(ENS_GX, None, None, "gy")),
        check_vma=False,
    )
```

profile of v0, /device:TPU:8, one launch (start us, length us, event | category | flops | bytes accessed | tf_op | source)
XLA Modules:
  0.0 1073.8 jit_solution(13558479619360328652)
XLA Ops:
  8.5 12.3 %all-to-all-start = ((bf16[1,75,256,128]{3,1,0,2:T(8,128)(2,1)}), bf16[1,75,256,128]{3,1,0,2:T(8,128)(2,1)}, u32[]{:S(2)}, u32[]{:S(2)}) async-start(bf16[1,75,256,128]{3,1,0,2:T(8,128)(2,1)} %copy.72), calls=%async_computation | async-start | bytes 10485760 | tf_op jit(solution)/shard_map/all_to_all | solution.py:107
  36.0 101.8 %collective-permute-done.2 = bf16[75,1,128]{0,2,1:T(8,128)(2,1)S(1)} collective-permute-done((bf16[75,1,128]{0,2,1:T(8,128)(2,1)S(1)}, bf16[75,1,128]{0,2,1:T(8,128)(2,1)S(1)}, u32[]{:S(2)}, u32[]{:S(2)}) %collective-permute-start.2) | collective-permute-done | bytes 19232 | tf_op jit(solution)/shard_map/ppermute | solution.py:26
  301.7 8.8 copy.131
  310.5 12.5 %reshape.178 = f32[64,75,512]{2,0,1:T(8,128)} reshape(f32[64,1,75,4,128]{4,3,0,2,1:T(4,128)} %bitcast.87) | data formatting | bytes 19660800 | tf_op jit(solution)/shard_map/convert_element_type | solution.py:113
  329.6 9.0 fusion.2
  341.1 22.0 %all-reduce.80 = (f32[]{:T(128)}, f32[]{:T(128)}) all-reduce(f32[]{:T(128)} %multiply_reduce_fusion.5, f32[]{:T(128)} %get-tuple-element.71), channel_id=1, replica_groups=mesh['ens_0'=2,'ens_1'=2,'gx_0'=4,'gx_1'=4,'gy'=4] {'ens_0'}, use_global_device_ids=true, to_apply=%region_1.2 | all-reduce | flops 2 | bytes 16 | tf_op jit(solution)/shard_map/psum | solution.py:39
  363.1 8.9 all-reduce.77
  380.3 11.2 %all-reduce.71 = (f32[]{:T(128)}, f32[]{:T(128)}) all-reduce(f32[]{:T(128)} %get-tuple-element.28, f32[]{:T(128)} %get-tuple-element.29), channel_id=1, replica_groups=mesh['ens_0'=2,'ens_1'=2,'gx_0'=4,'gx_1'=4,'gy'=4] {'gx_1'}, use_global_device_ids=true, to_apply=%region_4.5 | all-reduce | flops 2 | bytes 16 | tf_op jit(solution)/shard_map/psum | solution.py:39
  391.5 9.8 all-reduce.68
  555.5 8.4 collective-permute-start.81
  588.2 9.6 fusion.1
  601.7 14.7 %all-reduce.79 = (f32[]{:T(128)}, f32[]{:T(128)}) all-reduce(f32[]{:T(128)} %get-tuple-element.9, f32[]{:T(128)} %get-tuple-element.8), channel_id=1, replica_groups=mesh['ens_0'=2,'ens_1'=2,'gx_0'=4,'gx_1'=4,'gy'=4] {'ens_0'}, use_global_device_ids=true, to_apply=%region_17.18 | all-reduce | flops 2 | bytes 16 | tf_op jit(solution)/shard_map/psum | solution.py:39
  616.4 9.8 all-reduce.76
  626.2 8.3 all-reduce.73
  634.6 17.1 %all-reduce.70 = (f32[]{:T(128)}, f32[]{:T(128)}) all-reduce(f32[]{:T(128)} %get-tuple-element.26, f32[]{:T(128)} %get-tuple-element.27), channel_id=1, replica_groups=mesh['ens_0'=2,'ens_1'=2,'gx_0'=4,'gx_1'=4,'gy'=4] {'gx_1'}, use_global_device_ids=true, to_apply=%region_20.21 | all-reduce | flops 2 | bytes 16 | tf_op jit(solution)/shard_map/psum | solution.py:39
  651.7 9.8 all-reduce.67
  818.0 8.4 collective-permute-start.125
  850.6 9.6 fusion
  864.1 16.1 %all-reduce.78 = (f32[]{:T(128)}, f32[]{:T(128)}) all-reduce(f32[]{:T(128)} %get-tuple-element.11, f32[]{:T(128)} %get-tuple-element.10), channel_id=1, replica_groups=mesh['ens_0'=2,'ens_1'=2,'gx_0'=4,'gx_1'=4,'gy'=4] {'ens_0'}, use_global_device_ids=true, to_apply=%region_33.34 | all-reduce | flops 2 | bytes 16 | tf_op jit(solution)/shard_map/psum | solution.py:39
  886.5 8.4 all-reduce.72
  894.9 17.1 %all-reduce.69 = (f32[]{:T(128)}, f32[]{:T(128)}) all-reduce(f32[]{:T(128)} %get-tuple-element.24, f32[]{:T(128)} %get-tuple-element.25), channel_id=1, replica_groups=mesh['ens_0'=2,'ens_1'=2,'gx_0'=4,'gx_1'=4,'gy'=4] {'gx_1'}, use_global_device_ids=true, to_apply=%region_36.37 | all-reduce | flops 2 | bytes 16 | tf_op jit(solution)/shard_map/psum | solution.py:39
  912.0 10.0 all-reduce.66
  939.4 9.3 reshape.181
  955.1 111.1 %all-to-all-done.1 = bf16[64,75,4,128]{3,2,1,0:T(4,128)(2,1)} async-done(((bf16[64,75,4,128]{3,2,1,0:T(4,128)(2,1)}), bf16[64,75,4,128]{3,2,1,0:T(4,128)(2,1)}, u32[]{:S(2)}, u32[]{:S(2)}) %all-to-all-start.1) | async-done | bytes 4915232 | tf_op jit(solution)/shard_map/all_to_all | solution.py:148
  (455 shorter events, 596.7 us)
Async XLA Ops:
  8.5 293.1 %all-to-all-start = ((bf16[1,75,256,128]{3,1,0,2:T(8,128)(2,1)}), bf16[1,75,256,128]{3,1,0,2:T(8,128)(2,1)}, u32[]{:S(2)}, u32[]{:S(2)}) async-start(bf16[1,75,256,128]{3,1,0,2:T(8,128)(2,1)} %copy.72), calls=%async_computation | async-start | bytes 10485760 | tf_op jit(solution)/shard_map/all_to_all | solution.py:107
  21.3 116.4 %collective-permute-start.2 = (bf16[75,1,128]{0,2,1:T(8,128)(2,1)S(1)}, bf16[75,1,128]{0,2,1:T(8,128)(2,1)S(1)}, u32[]{:S(2)}, u32[]{:S(2)}) collective-permute-start(bf16[75,1,128]{0,2,1:T(8,128)(2,1)S(1)} %get-tuple-element.133), channel_id=1, source_target_pairs={{4,0},{8,4},{12,8},{16,12},{20,16},{24,20},{28,24},{32,28},{36,32}... | collective-permute-start | bytes 57608 | tf_op jit(solution)/shard_map/ppermute | solution.py:26
  22.6 115.1 %collective-permute-start.1 = (bf16[75,1,128]{0,2,1:T(8,128)(2,1)S(1)}, bf16[75,1,128]{0,2,1:T(8,128)(2,1)S(1)}, u32[]{:S(2)}, u32[]{:S(2)}) collective-permute-start(bf16[75,1,128]{0,2,1:T(8,128)(2,1)S(1)} %get-tuple-element.132), channel_id=1, source_target_pairs={{0,4},{4,8},{8,12},{12,16},{16,20},{20,24},{24,28},{28,32},{32,36}... | collective-permute-start | bytes 57608 | tf_op jit(solution)/shard_map/ppermute | solution.py:25
  184.8 17.4 %collective-permute-start.16 = (f32[75,1,32]{0,2,1:T(8,128)S(1)}, f32[75,1,32]{0,2,1:T(8,128)S(1)}, u32[]{:S(2)}, u32[]{:S(2)}) collective-permute-start(f32[75,1,32]{0,2,1:T(8,128)S(1)} %multiply_bitcast_fusion.2), channel_id=1, source_target_pairs={{4,0},{8,4},{12,8},{16,12},{20,16},{24,20},{28,24},{32,28},{36,32}... | collective-permute-start | bytes 28808 | tf_op jit(solution)/shard_map/ppermute | solution.py:26
  202.2 17.4 %collective-permute-start.20 = (f32[75,1,32]{0,2,1:T(8,128)S(1)}, f32[75,1,32]{0,2,1:T(8,128)S(1)}, u32[]{:S(2)}, u32[]{:S(2)}) collective-permute-start(f32[75,1,32]{0,2,1:T(8,128)S(1)} %fusion.369), channel_id=1, source_target_pairs={{4,0},{8,4},{12,8},{16,12},{20,16},{24,20},{28,24},{32,28},{36,32}... | collective-permute-start | bytes 28808 | tf_op jit(solution)/shard_map/ppermute | solution.py:26
  235.0 17.4 %collective-permute-start.30 = (bf16[75,1,64]{0,2,1:T(8,128)(2,1)S(1)}, bf16[75,1,64]{0,2,1:T(8,128)(2,1)S(1)}, u32[]{:S(2)}, u32[]{:S(2)}) collective-permute-start(bf16[75,1,64]{0,2,1:T(8,128)(2,1)S(1)} %get-tuple-element.173), channel_id=1, source_target_pairs={{4,0},{8,4},{12,8},{16,12},{20,16},{24,20},{28,24},{32,28},{36,32}... | collective-permute-start | bytes 28808 | tf_op jit(solution)/shard_map/ppermute | solution.py:26
  462.8 17.6 %collective-permute-start.60 = (f32[75,1,32]{0,2,1:T(8,128)S(1)}, f32[75,1,32]{0,2,1:T(8,128)S(1)}, u32[]{:S(2)}, u32[]{:S(2)}) collective-permute-start(f32[75,1,32]{0,2,1:T(8,128)S(1)} %multiply_bitcast_fusion.1), channel_id=1, source_target_pairs={{4,0},{8,4},{12,8},{16,12},{20,16},{24,20},{28,24},{32,28},{36,32}... | collective-permute-start | bytes 28808 | tf_op jit(solution)/shard_map/ppermute | solution.py:26
  480.4 17.4 %collective-permute-start.64 = (f32[75,1,32]{0,2,1:T(8,128)S(1)}, f32[75,1,32]{0,2,1:T(8,128)S(1)}, u32[]{:S(2)}, u32[]{:S(2)}) collective-permute-start(f32[75,1,32]{0,2,1:T(8,128)S(1)} %fusion.341), channel_id=1, source_target_pairs={{4,0},{8,4},{12,8},{16,12},{20,16},{24,20},{28,24},{32,28},{36,32}... | collective-permute-start | bytes 28808 | tf_op jit(solution)/shard_map/ppermute | solution.py:26
  513.3 17.4 %collective-permute-start.74 = (bf16[75,1,64]{0,2,1:T(8,128)(2,1)S(1)}, bf16[75,1,64]{0,2,1:T(8,128)(2,1)S(1)}, u32[]{:S(2)}, u32[]{:S(2)}) collective-permute-start(bf16[75,1,64]{0,2,1:T(8,128)(2,1)S(1)} %get-tuple-element.157), channel_id=1, source_target_pairs={{4,0},{8,4},{12,8},{16,12},{20,16},{24,20},{28,24},{32,28},{36,32}... | collective-permute-start | bytes 28808 | tf_op jit(solution)/shard_map/ppermute | solution.py:26
  548.4 21.2 %collective-permute-start.83 = (bf16[75,4,1]{0,2,1:T(2,128)(2,1)}, bf16[75,4,1]{0,2,1:T(2,128)(2,1)S(1)}, u32[]{:S(2)}, u32[]{:S(2)}) collective-permute-start(bf16[75,4,1]{0,2,1:T(2,128)(2,1)} %get-tuple-element.111), channel_id=1, source_target_pairs={{1,0},{2,1},{3,2},{5,4},{6,5},{7,6},{9,8},{10,9},{11,10},{13,12},{... | collective-permute-start | bytes 1808 | tf_op jit(solution)/shard_map/ppermute | solution.py:26
  550.3 19.3 %collective-permute-start.80 = (bf16[75,4,1]{0,2,1:T(2,128)(2,1)}, bf16[75,4,1]{0,2,1:T(2,128)(2,1)}, u32[]{:S(2)}, u32[]{:S(2)}) collective-permute-start(bf16[75,4,1]{0,2,1:T(2,128)(2,1)} %get-tuple-element.110), channel_id=1, source_target_pairs={{0,1},{1,2},{2,3},{4,5},{5,6},{6,7},{8,9},{9,10},{10,11},{12,13},{... | collective-permute-start | bytes 1808 | tf_op jit(solution)/shard_map/ppermute | solution.py:25
  573.5 25.4 %collective-permute-start.87 = (bf16[75,4,1]{0,2,1:T(2,128)(2,1)}, bf16[75,4,1]{0,2,1:T(2,128)(2,1)S(1)}, u32[]{:S(2)}, u32[]{:S(2)}) collective-permute-start(bf16[75,4,1]{0,2,1:T(2,128)(2,1)} %get-tuple-element.107), channel_id=1, source_target_pairs={{1,0},{2,1},{3,2},{5,4},{6,5},{7,6},{9,8},{10,9},{11,10},{13,12},{... | collective-permute-start | bytes 1808 | tf_op jit(solution)/shard_map/ppermute | solution.py:26
  575.9 23.0 %collective-permute-start.84 = (bf16[75,4,1]{0,2,1:T(2,128)(2,1)}, bf16[75,4,1]{0,2,1:T(2,128)(2,1)}, u32[]{:S(2)}, u32[]{:S(2)}) collective-permute-start(bf16[75,4,1]{0,2,1:T(2,128)(2,1)} %get-tuple-element.106), channel_id=1, source_target_pairs={{0,1},{1,2},{2,3},{4,5},{5,6},{6,7},{8,9},{9,10},{10,11},{12,13},{... | collective-permute-start | bytes 1808 | tf_op jit(solution)/shard_map/ppermute | solution.py:25
  579.3 19.6 %collective-permute-start.86 = (bf16[75,1,128]{0,2,1:T(8,128)(2,1)}, bf16[75,1,128]{0,2,1:T(8,128)(2,1)S(1)}, u32[]{:S(2)}, u32[]{:S(2)}) collective-permute-start(bf16[75,1,128]{0,2,1:T(8,128)(2,1)} %get-tuple-element.105), channel_id=1, source_target_pairs={{4,0},{8,4},{12,8},{16,12},{20,16},{24,20},{28,24},{32,28},{36,32}... | collective-permute-start | bytes 57608 | tf_op jit(solution)/shard_map/ppermute | solution.py:26
  580.6 18.3 %collective-permute-start.85 = (bf16[75,1,128]{0,2,1:T(8,128)(2,1)}, bf16[75,1,128]{0,2,1:T(8,128)(2,1)}, u32[]{:S(2)}, u32[]{:S(2)}) collective-permute-start(bf16[75,1,128]{0,2,1:T(8,128)(2,1)} %get-tuple-element.104), channel_id=1, source_target_pairs={{0,4},{4,8},{8,12},{12,16},{16,20},{20,24},{24,28},{28,32},{32,36}... | collective-permute-start | bytes 57608 | tf_op jit(solution)/shard_map/ppermute | solution.py:25
  741.9 17.4 %collective-permute-start.108 = (f32[75,1,32]{0,2,1:T(8,128)S(1)}, f32[75,1,32]{0,2,1:T(8,128)S(1)}, u32[]{:S(2)}, u32[]{:S(2)}) collective-permute-start(f32[75,1,32]{0,2,1:T(8,128)S(1)} %fusion.313), channel_id=1, source_target_pairs={{4,0},{8,4},{12,8},{16,12},{20,16},{24,20},{28,24},{32,28},{36,32}... | collective-permute-start | bytes 28808 | tf_op jit(solution)/shard_map/ppermute | solution.py:26
  774.8 17.5 %collective-permute-start.118 = (bf16[75,1,64]{0,2,1:T(8,128)(2,1)S(1)}, bf16[75,1,64]{0,2,1:T(8,128)(2,1)S(1)}, u32[]{:S(2)}, u32[]{:S(2)}) collective-permute-start(bf16[75,1,64]{0,2,1:T(8,128)(2,1)S(1)} %get-tuple-element.141), channel_id=1, source_target_pairs={{4,0},{8,4},{12,8},{16,12},{20,16},{24,20},{28,24},{32,28},{36,32}... | collective-permute-start | bytes 28808 | tf_op jit(solution)/shard_map/ppermute | solution.py:26
  810.8 21.1 %collective-permute-start.127 = (bf16[75,4,1]{0,2,1:T(2,128)(2,1)}, bf16[75,4,1]{0,2,1:T(2,128)(2,1)S(1)}, u32[]{:S(2)}, u32[]{:S(2)}) collective-permute-start(bf16[75,4,1]{0,2,1:T(2,128)(2,1)} %get-tuple-element.95), channel_id=1, source_target_pairs={{1,0},{2,1},{3,2},{5,4},{6,5},{7,6},{9,8},{10,9},{11,10},{13,12},{... | collective-permute-start | bytes 1808 | tf_op jit(solution)/shard_map/ppermute | solution.py:26
  812.7 19.2 %collective-permute-start.124 = (bf16[75,4,1]{0,2,1:T(2,128)(2,1)}, bf16[75,4,1]{0,2,1:T(2,128)(2,1)}, u32[]{:S(2)}, u32[]{:S(2)}) collective-permute-start(bf16[75,4,1]{0,2,1:T(2,128)(2,1)} %get-tuple-element.94), channel_id=1, source_target_pairs={{0,1},{1,2},{2,3},{4,5},{5,6},{6,7},{8,9},{9,10},{10,11},{12,13},{... | collective-permute-start | bytes 1808 | tf_op jit(solution)/shard_map/ppermute | solution.py:25
  835.9 25.4 %collective-permute-start.131 = (bf16[75,4,1]{0,2,1:T(2,128)(2,1)}, bf16[75,4,1]{0,2,1:T(2,128)(2,1)S(1)}, u32[]{:S(2)}, u32[]{:S(2)}) collective-permute-start(bf16[75,4,1]{0,2,1:T(2,128)(2,1)} %get-tuple-element.91), channel_id=1, source_target_pairs={{1,0},{2,1},{3,2},{5,4},{6,5},{7,6},{9,8},{10,9},{11,10},{13,12},{... | collective-permute-start | bytes 1808 | tf_op jit(solution)/shard_map/ppermute | solution.py:26
  838.3 23.0 %collective-permute-start.128 = (bf16[75,4,1]{0,2,1:T(2,128)(2,1)}, bf16[75,4,1]{0,2,1:T(2,128)(2,1)}, u32[]{:S(2)}, u32[]{:S(2)}) collective-permute-start(bf16[75,4,1]{0,2,1:T(2,128)(2,1)} %get-tuple-element.90), channel_id=1, source_target_pairs={{0,1},{1,2},{2,3},{4,5},{5,6},{6,7},{8,9},{9,10},{10,11},{12,13},{... | collective-permute-start | bytes 1808 | tf_op jit(solution)/shard_map/ppermute | solution.py:25
  841.7 19.6 %collective-permute-start.130 = (bf16[75,1,128]{0,2,1:T(8,128)(2,1)}, bf16[75,1,128]{0,2,1:T(8,128)(2,1)S(1)}, u32[]{:S(2)}, u32[]{:S(2)}) collective-permute-start(bf16[75,1,128]{0,2,1:T(8,128)(2,1)} %get-tuple-element.89), channel_id=1, source_target_pairs={{4,0},{8,4},{12,8},{16,12},{20,16},{24,20},{28,24},{32,28},{36,32}... | collective-permute-start | bytes 57608 | tf_op jit(solution)/shard_map/ppermute | solution.py:26
  843.0 18.3 %collective-permute-start.129 = (bf16[75,1,128]{0,2,1:T(8,128)(2,1)}, bf16[75,1,128]{0,2,1:T(8,128)(2,1)}, u32[]{:S(2)}, u32[]{:S(2)}) collective-permute-start(bf16[75,1,128]{0,2,1:T(8,128)(2,1)} %get-tuple-element.88), channel_id=1, source_target_pairs={{0,4},{4,8},{8,12},{12,16},{16,20},{20,24},{24,28},{28,32},{32,36}... | collective-permute-start | bytes 57608 | tf_op jit(solution)/shard_map/ppermute | solution.py:25
  948.6 117.5 %all-to-all-start.1 = ((bf16[64,75,4,128]{3,2,1,0:T(4,128)(2,1)}), bf16[64,75,4,128]{3,2,1,0:T(4,128)(2,1)}, u32[]{:S(2)}, u32[]{:S(2)}) async-start(bf16[64,75,4,128]{3,2,1,0:T(4,128)(2,1)} %reshape.181), calls=%async_computation.1 | async-start | bytes 9830400 | tf_op jit(solution)/shard_map/all_to_all | solution.py:148
  (123 other events, 1926.2 us)
where the time goes:
time: 1090 us; the launch traced here: 1070 us
  starting transfers between devices  471 us (43%)
  waiting for transfers between devices  274 us (25%)
  blocking collectives  178 us (16%)
  local copies, waits for them, and re-layouts  57.6 us (5%)
  other arithmetic  45 us (4%)
  matrix products  34.7 us (3%)
  between operations  12.9 us (1%)
    ppermute x66, starting transfers between devices, padded_2(): lax.ppermute(last, axis, up)  332 us
    psum x15, blocking collectives, by_axis(): x = lax.psum(x, axis)  178 us
    ppermute x66, waiting for transfers between devices, padded_2(): lax.ppermute(leading, axis, [(b, a) for a, b in up])  127 us
    ppermute x66, starting transfers between devices, padded_2(): lax.ppermute(leading, axis, [(b, a) for a, b in up])  122 us
    all_to_all x1, waiting for transfers between devices, local(): lax.all_to_all(final, ENS_GX, split_axis=0, concat_axis=2, tiled=True)  111 us
    ppermute x66, waiting for transfers between devices, padded_2(): lax.ppermute(last, axis, up)  36.1 us
    dot_general x4, matrix products, member_products(): jnp.einsum('ij,kjc->kic', spread, flat, preferred_element_type=jnp.float32)  34.7 us
    convert_element_type x4, other arithmetic, member_products(): product = (tiles * masked).astype(jnp.bfloat16)  22.4 us
  transfers between devices with their start and end apart: 134, of which 31 were waited for; matrix products, arithmetic and copies ran while one was open for 4% of the time, Pallas kernels for 0%

commit v1 on v0

--- a/solution.py
+++ b/solution.py
@@ -36,7 +36,7 @@
 
 def by_axis(x, axes):
     for axis in axes:
-        x = lax.psum(x, axis)
+        x = jnp.sum(lax.all_gather(x, axis), 0)
     return x
 
 

time: 1090 us -> 1140 us (1.046)
  local copies, waits for them, and re-layouts: 57.6 us -> 103 us
  other arithmetic: 45 us -> 63.2 us
  blocking collectives: 178 us -> 166 us
    psum x15 -> x0, blocking collectives: 178 us -> none  [by_axis(): x = lax.psum(x, axis)]
    unnamed x0 -> x15, blocking collectives: none -> 166 us
    unnamed x31 -> x106, local copies, waits for them, and re-layouts: 10.1 us -> 55.3 us
    reduce_sum x0 -> x30, other arithmetic: none -> 18.2 us  [by_axis(): x = jnp.sum(lax.all_gather(x, axis), 0)]
  transfers between devices with their start and end apart: 134 -> 134, of which waited for: 31 -> 30; matrix products, arithmetic and copies ran while one was open for 4% -> 4% of each run, Pallas kernels for 0% -> 0%
where the time goes in v1:
time: 1140 us; the launch traced here: 1120 us
  starting transfers between devices  470 us (41%)
  waiting for transfers between devices  275 us (24%)
  blocking collectives  166 us (15%)
  local copies, waits for them, and re-layouts  103 us (9%)
  other arithmetic  63.2 us (6%)
  matrix products  34.7 us (3%)
  between operations  13.3 us (1%)
    ppermute x66, starting transfers between devices, padded_2(): lax.ppermute(last, axis, up)  329 us
    unnamed x15, blocking collectives  166 us
    ppermute x66, waiting for transfers between devices, padded_2(): lax.ppermute(leading, axis, [(b, a) for a, b in up])  127 us
    ppermute x66, starting transfers between devices, padded_2(): lax.ppermute(leading, axis, [(b, a) for a, b in up])  123 us
    all_to_all x1, waiting for transfers between devices, local(): lax.all_to_all(final, ENS_GX, split_axis=0, concat_axis=2, tiled=True)  111 us
    unnamed x106, local copies, waits for them, and re-layouts  55.3 us
    ppermute x66, waiting for transfers between devices, padded_2(): lax.ppermute(last, axis, up)  36 us
    dot_general x4, matrix products, member_products(): jnp.einsum('ij,kjc->kic', spread, flat, preferred_element_type=jnp.float32)  34.7 us
  transfers between devices with their start and end apart: 134, of which 30 were waited for; matrix products, arithmetic and copies ran while one was open for 4% of the time, Pallas kernels for 0%

profile of v1, /device:TPU:8, one launch (start us, length us, event | category | flops | bytes accessed | tf_op | source)
XLA Modules:
  0.0 1124.3 jit_solution(243036867034139875)
XLA Ops:
  0.6 8.0 copy.72
  8.7 12.3 %all-to-all-start = ((bf16[1,75,256,128]{3,1,0,2:T(8,128)(2,1)}), bf16[1,75,256,128]{3,1,0,2:T(8,128)(2,1)}, u32[]{:S(2)}, u32[]{:S(2)}) async-start(bf16[1,75,256,128]{3,1,0,2:T(8,128)(2,1)} %copy.72), calls=%async_computation | async-start | bytes 10485760 | tf_op jit(solution)/shard_map/all_to_all | solution.py:107
  36.2 101.6 %collective-permute-done.2 = bf16[75,1,128]{0,2,1:T(8,128)(2,1)S(1)} collective-permute-done((bf16[75,1,128]{0,2,1:T(8,128)(2,1)S(1)}, bf16[75,1,128]{0,2,1:T(8,128)(2,1)S(1)}, u32[]{:S(2)}, u32[]{:S(2)}) %collective-permute-start.2) | collective-permute-done | bytes 19232 | tf_op jit(solution)/shard_map/ppermute | solution.py:26
  302.2 8.8 copy.131
  311.0 12.5 %reshape.178 = f32[64,75,512]{2,0,1:T(8,128)} reshape(f32[64,1,75,4,128]{4,3,0,2,1:T(4,128)} %bitcast.122) | data formatting | bytes 19660800 | tf_op jit(solution)/shard_map/convert_element_type | solution.py:113
  330.1 9.0 fusion.2
  343.6 16.1 %all-reduce.110 = (f32[2]{0:T(128)S(1)}, f32[2]{0:T(128)S(1)}) all-reduce(f32[2]{0:T(128)S(1)} %dynamic-update-slice, f32[2]{0:T(128)S(1)} %dynamic-update-slice.5), channel_id=1, replica_groups=mesh['ens_0'=2,'ens_1'=2,'gx_0'=4,'gx_1'=4,'gy'=4] {'ens_0'}, use_global_device_ids=true, to_apply=%add.66 | all-reduce | flops 4 | bytes 32
  388.7 16.8 %all-reduce.101 = (f32[4]{0:T(128)S(1)}, f32[4]{0:T(128)S(1)}) all-reduce(f32[4]{0:T(128)S(1)} %dynamic-update-slice.3, f32[4]{0:T(128)S(1)} %dynamic-update-slice.8), channel_id=1, replica_groups=mesh['ens_0'=2,'ens_1'=2,'gx_0'=4,'gx_1'=4,'gy'=4] {'gx_1'}, use_global_device_ids=true, to_apply=%add.69 | all-reduce | flops 8 | bytes 64
  409.4 9.1 all-reduce.98
  574.3 8.4 collective-permute-start.81
  607.0 9.6 fusion.1
  623.0 15.4 %all-reduce.109 = (f32[2]{0:T(128)S(1)}, f32[2]{0:T(128)S(1)}) all-reduce(f32[2]{0:T(128)S(1)} %dynamic-update-slice.10, f32[2]{0:T(128)S(1)} %dynamic-update-slice.15), channel_id=1, replica_groups=mesh['ens_0'=2,'ens_1'=2,'gx_0'=4,'gx_1'=4,'gy'=4] {'ens_0'}, use_global_device_ids=true, to_apply=%add.76 | all-reduce | flops 4 | bytes 32
  652.4 7.7 all-reduce.103
  664.1 16.5 %all-reduce.100 = (f32[4]{0:T(128)S(1)}, f32[4]{0:T(128)S(1)}) all-reduce(f32[4]{0:T(128)S(1)} %dynamic-update-slice.13, f32[4]{0:T(128)S(1)} %dynamic-update-slice.18), channel_id=1, replica_groups=mesh['ens_0'=2,'ens_1'=2,'gx_0'=4,'gx_1'=4,'gy'=4] {'gx_1'}, use_global_device_ids=true, to_apply=%add.79 | all-reduce | flops 8 | bytes 64
  684.5 9.1 all-reduce.97
  851.6 8.4 collective-permute-start.125
  876.7 7.7 collective-permute-start.129
  884.4 9.6 fusion
  900.6 15.4 %all-reduce.108 = (f32[2]{0:T(128)S(1)}, f32[2]{0:T(128)S(1)}) all-reduce(f32[2]{0:T(128)S(1)} %dynamic-update-slice.20, f32[2]{0:T(128)S(1)} %dynamic-update-slice.25), channel_id=1, replica_groups=mesh['ens_0'=2,'ens_1'=2,'gx_0'=4,'gx_1'=4,'gy'=4] {'ens_0'}, use_global_device_ids=true, to_apply=%add.86 | all-reduce | flops 4 | bytes 32
  929.7 7.7 all-reduce.102
  941.4 16.5 %all-reduce.99 = (f32[4]{0:T(128)S(1)}, f32[4]{0:T(128)S(1)}) all-reduce(f32[4]{0:T(128)S(1)} %dynamic-update-slice.23, f32[4]{0:T(128)S(1)} %dynamic-update-slice.28), channel_id=1, replica_groups=mesh['ens_0'=2,'ens_1'=2,'gx_0'=4,'gx_1'=4,'gy'=4] {'gx_1'}, use_global_device_ids=true, to_apply=%add.89 | all-reduce | flops 8 | bytes 64
  961.8 9.3 all-reduce.96
  989.9 9.3 reshape.331
  1005.6 111.1 %all-to-all-done.1 = bf16[64,75,4,128]{3,2,1,0:T(4,128)(2,1)} async-done(((bf16[64,75,4,128]{3,2,1,0:T(4,128)(2,1)}), bf16[64,75,4,128]{3,2,1,0:T(4,128)(2,1)}, u32[]{:S(2)}, u32[]{:S(2)}) %all-to-all-start.1) | async-done | bytes 4915232 | tf_op jit(solution)/shard_map/all_to_all | solution.py:148
  (560 shorter events, 655.0 us)
Async XLA Ops:
  8.7 293.5 %all-to-all-start = ((bf16[1,75,256,128]{3,1,0,2:T(8,128)(2,1)}), bf16[1,75,256,128]{3,1,0,2:T(8,128)(2,1)}, u32[]{:S(2)}, u32[]{:S(2)}) async-start(bf16[1,75,256,128]{3,1,0,2:T(8,128)(2,1)} %copy.72), calls=%async_computation | async-start | bytes 10485760 | tf_op jit(solution)/shard_map/all_to_all | solution.py:107
  21.5 116.4 %collective-permute-start.2 = (bf16[75,1,128]{0,2,1:T(8,128)(2,1)S(1)}, bf16[75,1,128]{0,2,1:T(8,128)(2,1)S(1)}, u32[]{:S(2)}, u32[]{:S(2)}) collective-permute-start(bf16[75,1,128]{0,2,1:T(8,128)(2,1)S(1)} %get-tuple-element.133), channel_id=1, source_target_pairs={{4,0},{8,4},{12,8},{16,12},{20,16},{24,20},{28,24},{32,28},{36,32}... | collective-permute-start | bytes 57608 | tf_op jit(solution)/shard_map/ppermute | solution.py:26
  22.9 114.9 %collective-permute-start.1 = (bf16[75,1,128]{0,2,1:T(8,128)(2,1)S(1)}, bf16[75,1,128]{0,2,1:T(8,128)(2,1)S(1)}, u32[]{:S(2)}, u32[]{:S(2)}) collective-permute-start(bf16[75,1,128]{0,2,1:T(8,128)(2,1)S(1)} %get-tuple-element.132), channel_id=1, source_target_pairs={{0,4},{4,8},{8,12},{12,16},{16,20},{20,24},{24,28},{28,32},{32,36}... | collective-permute-start | bytes 57608 | tf_op jit(solution)/shard_map/ppermute | solution.py:25
  184.8 17.4 %collective-permute-start.16 = (f32[75,1,32]{0,2,1:T(8,128)S(1)}, f32[75,1,32]{0,2,1:T(8,128)S(1)}, u32[]{:S(2)}, u32[]{:S(2)}) collective-permute-start(f32[75,1,32]{0,2,1:T(8,128)S(1)} %multiply_bitcast_fusion.2), channel_id=1, source_target_pairs={{4,0},{8,4},{12,8},{16,12},{20,16},{24,20},{28,24},{32,28},{36,32}... | collective-permute-start | bytes 28808 | tf_op jit(solution)/shard_map/ppermute | solution.py:26
  202.2 17.4 %collective-permute-start.20 = (f32[75,1,32]{0,2,1:T(8,128)S(1)}, f32[75,1,32]{0,2,1:T(8,128)S(1)}, u32[]{:S(2)}, u32[]{:S(2)}) collective-permute-start(f32[75,1,32]{0,2,1:T(8,128)S(1)} %fusion.369), channel_id=1, source_target_pairs={{4,0},{8,4},{12,8},{16,12},{20,16},{24,20},{28,24},{32,28},{36,32}... | collective-permute-start | bytes 28808 | tf_op jit(solution)/shard_map/ppermute | solution.py:26
  235.0 17.4 %collective-permute-start.30 = (bf16[75,1,64]{0,2,1:T(8,128)(2,1)S(1)}, bf16[75,1,64]{0,2,1:T(8,128)(2,1)S(1)}, u32[]{:S(2)}, u32[]{:S(2)}) collective-permute-start(bf16[75,1,64]{0,2,1:T(8,128)(2,1)S(1)} %get-tuple-element.173), channel_id=1, source_target_pairs={{4,0},{8,4},{12,8},{16,12},{20,16},{24,20},{28,24},{32,28},{36,32}... | collective-permute-start | bytes 28808 | tf_op jit(solution)/shard_map/ppermute | solution.py:26
  284.4 17.0 %collective-permute-start.42 = (bf16[75,1,128]{0,2,1:T(8,128)(2,1)S(1)}, bf16[75,1,128]{0,2,1:T(8,128)(2,1)S(1)}, u32[]{:S(2)}, u32[]{:S(2)}) collective-permute-start(bf16[75,1,128]{0,2,1:T(8,128)(2,1)S(1)} %get-tuple-element.121), channel_id=1, source_target_pairs={{4,0},{8,4},{12,8},{16,12},{20,16},{24,20},{28,24},{32,28},{36,32}... | collective-permute-start | bytes 57608 | tf_op jit(solution)/shard_map/ppermute | solution.py:26
  498.3 17.4 %collective-permute-start.64 = (f32[75,1,32]{0,2,1:T(8,128)S(1)}, f32[75,1,32]{0,2,1:T(8,128)S(1)}, u32[]{:S(2)}, u32[]{:S(2)}) collective-permute-start(f32[75,1,32]{0,2,1:T(8,128)S(1)} %fusion.341), channel_id=1, source_target_pairs={{4,0},{8,4},{12,8},{16,12},{20,16},{24,20},{28,24},{32,28},{36,32}... | collective-permute-start | bytes 28808 | tf_op jit(solution)/shard_map/ppermute | solution.py:26
  531.1 17.5 %collective-permute-start.74 = (bf16[75,1,64]{0,2,1:T(8,128)(2,1)S(1)}, bf16[75,1,64]{0,2,1:T(8,128)(2,1)S(1)}, u32[]{:S(2)}, u32[]{:S(2)}) collective-permute-start(bf16[75,1,64]{0,2,1:T(8,128)(2,1)S(1)} %get-tuple-element.157), channel_id=1, source_target_pairs={{4,0},{8,4},{12,8},{16,12},{20,16},{24,20},{28,24},{32,28},{36,32}... | collective-permute-start | bytes 28808 | tf_op jit(solution)/shard_map/ppermute | solution.py:26
  567.2 21.2 %collective-permute-start.83 = (bf16[75,4,1]{0,2,1:T(2,128)(2,1)}, bf16[75,4,1]{0,2,1:T(2,128)(2,1)S(1)}, u32[]{:S(2)}, u32[]{:S(2)}) collective-permute-start(bf16[75,4,1]{0,2,1:T(2,128)(2,1)} %get-tuple-element.111), channel_id=1, source_target_pairs={{1,0},{2,1},{3,2},{5,4},{6,5},{7,6},{9,8},{10,9},{11,10},{13,12},{... | collective-permute-start | bytes 1808 | tf_op jit(solution)/shard_map/ppermute | solution.py:26
  569.1 19.3 %collective-permute-start.80 = (bf16[75,4,1]{0,2,1:T(2,128)(2,1)}, bf16[75,4,1]{0,2,1:T(2,128)(2,1)}, u32[]{:S(2)}, u32[]{:S(2)}) collective-permute-start(bf16[75,4,1]{0,2,1:T(2,128)(2,1)} %get-tuple-element.110), channel_id=1, source_target_pairs={{0,1},{1,2},{2,3},{4,5},{5,6},{6,7},{8,9},{9,10},{10,11},{12,13},{... | collective-permute-start | bytes 1808 | tf_op jit(solution)/shard_map/ppermute | solution.py:25
  592.2 25.4 %collective-permute-start.87 = (bf16[75,4,1]{0,2,1:T(2,128)(2,1)}, bf16[75,4,1]{0,2,1:T(2,128)(2,1)S(1)}, u32[]{:S(2)}, u32[]{:S(2)}) collective-permute-start(bf16[75,4,1]{0,2,1:T(2,128)(2,1)} %get-tuple-element.107), channel_id=1, source_target_pairs={{1,0},{2,1},{3,2},{5,4},{6,5},{7,6},{9,8},{10,9},{11,10},{13,12},{... | collective-permute-start | bytes 1808 | tf_op jit(solution)/shard_map/ppermute | solution.py:26
  594.7 23.0 %collective-permute-start.84 = (bf16[75,4,1]{0,2,1:T(2,128)(2,1)}, bf16[75,4,1]{0,2,1:T(2,128)(2,1)}, u32[]{:S(2)}, u32[]{:S(2)}) collective-permute-start(bf16[75,4,1]{0,2,1:T(2,128)(2,1)} %get-tuple-element.106), channel_id=1, source_target_pairs={{0,1},{1,2},{2,3},{4,5},{5,6},{6,7},{8,9},{9,10},{10,11},{12,13},{... | collective-permute-start | bytes 1808 | tf_op jit(solution)/shard_map/ppermute | solution.py:25
  598.1 19.6 %collective-permute-start.86 = (bf16[75,1,128]{0,2,1:T(8,128)(2,1)}, bf16[75,1,128]{0,2,1:T(8,128)(2,1)S(1)}, u32[]{:S(2)}, u32[]{:S(2)}) collective-permute-start(bf16[75,1,128]{0,2,1:T(8,128)(2,1)} %get-tuple-element.105), channel_id=1, source_target_pairs={{4,0},{8,4},{12,8},{16,12},{20,16},{24,20},{28,24},{32,28},{36,32}... | collective-permute-start | bytes 57608 | tf_op jit(solution)/shard_map/ppermute | solution.py:26
  599.4 18.3 %collective-permute-start.85 = (bf16[75,1,128]{0,2,1:T(8,128)(2,1)}, bf16[75,1,128]{0,2,1:T(8,128)(2,1)}, u32[]{:S(2)}, u32[]{:S(2)}) collective-permute-start(bf16[75,1,128]{0,2,1:T(8,128)(2,1)} %get-tuple-element.104), channel_id=1, source_target_pairs={{0,4},{4,8},{8,12},{12,16},{16,20},{20,24},{24,28},{28,32},{32,36}... | collective-permute-start | bytes 57608 | tf_op jit(solution)/shard_map/ppermute | solution.py:25
  775.6 17.4 %collective-permute-start.108 = (f32[75,1,32]{0,2,1:T(8,128)S(1)}, f32[75,1,32]{0,2,1:T(8,128)S(1)}, u32[]{:S(2)}, u32[]{:S(2)}) collective-permute-start(f32[75,1,32]{0,2,1:T(8,128)S(1)} %fusion.313), channel_id=1, source_target_pairs={{4,0},{8,4},{12,8},{16,12},{20,16},{24,20},{28,24},{32,28},{36,32}... | collective-permute-start | bytes 28808 | tf_op jit(solution)/shard_map/ppermute | solution.py:26
  808.5 17.5 %collective-permute-start.118 = (bf16[75,1,64]{0,2,1:T(8,128)(2,1)S(1)}, bf16[75,1,64]{0,2,1:T(8,128)(2,1)S(1)}, u32[]{:S(2)}, u32[]{:S(2)}) collective-permute-start(bf16[75,1,64]{0,2,1:T(8,128)(2,1)S(1)} %get-tuple-element.141), channel_id=1, source_target_pairs={{4,0},{8,4},{12,8},{16,12},{20,16},{24,20},{28,24},{32,28},{36,32}... | collective-permute-start | bytes 28808 | tf_op jit(solution)/shard_map/ppermute | solution.py:26
  844.5 21.2 %collective-permute-start.127 = (bf16[75,4,1]{0,2,1:T(2,128)(2,1)}, bf16[75,4,1]{0,2,1:T(2,128)(2,1)S(1)}, u32[]{:S(2)}, u32[]{:S(2)}) collective-permute-start(bf16[75,4,1]{0,2,1:T(2,128)(2,1)} %get-tuple-element.95), channel_id=1, source_target_pairs={{1,0},{2,1},{3,2},{5,4},{6,5},{7,6},{9,8},{10,9},{11,10},{13,12},{... | collective-permute-start | bytes 1808 | tf_op jit(solution)/shard_map/ppermute | solution.py:26
  846.4 19.3 %collective-permute-start.124 = (bf16[75,4,1]{0,2,1:T(2,128)(2,1)}, bf16[75,4,1]{0,2,1:T(2,128)(2,1)}, u32[]{:S(2)}, u32[]{:S(2)}) collective-permute-start(bf16[75,4,1]{0,2,1:T(2,128)(2,1)} %get-tuple-element.94), channel_id=1, source_target_pairs={{0,1},{1,2},{2,3},{4,5},{5,6},{6,7},{8,9},{9,10},{10,11},{12,13},{... | collective-permute-start | bytes 1808 | tf_op jit(solution)/shard_map/ppermute | solution.py:25
  869.5 25.6 %collective-permute-start.131 = (bf16[75,4,1]{0,2,1:T(2,128)(2,1)}, bf16[75,4,1]{0,2,1:T(2,128)(2,1)S(1)}, u32[]{:S(2)}, u32[]{:S(2)}) collective-permute-start(bf16[75,4,1]{0,2,1:T(2,128)(2,1)} %get-tuple-element.91), channel_id=1, source_target_pairs={{1,0},{2,1},{3,2},{5,4},{6,5},{7,6},{9,8},{10,9},{11,10},{13,12},{... | collective-permute-start | bytes 1808 | tf_op jit(solution)/shard_map/ppermute | solution.py:26
  872.0 23.1 %collective-permute-start.128 = (bf16[75,4,1]{0,2,1:T(2,128)(2,1)}, bf16[75,4,1]{0,2,1:T(2,128)(2,1)}, u32[]{:S(2)}, u32[]{:S(2)}) collective-permute-start(bf16[75,4,1]{0,2,1:T(2,128)(2,1)} %get-tuple-element.90), channel_id=1, source_target_pairs={{0,1},{1,2},{2,3},{4,5},{5,6},{6,7},{8,9},{9,10},{10,11},{12,13},{... | collective-permute-start | bytes 1808 | tf_op jit(solution)/shard_map/ppermute | solution.py:25
  875.4 19.8 %collective-permute-start.130 = (bf16[75,1,128]{0,2,1:T(8,128)(2,1)}, bf16[75,1,128]{0,2,1:T(8,128)(2,1)S(1)}, u32[]{:S(2)}, u32[]{:S(2)}) collective-permute-start(bf16[75,1,128]{0,2,1:T(8,128)(2,1)} %get-tuple-element.89), channel_id=1, source_target_pairs={{4,0},{8,4},{12,8},{16,12},{20,16},{24,20},{28,24},{32,28},{36,32}... | collective-permute-start | bytes 57608 | tf_op jit(solution)/shard_map/ppermute | solution.py:26
  876.7 18.5 %collective-permute-start.129 = (bf16[75,1,128]{0,2,1:T(8,128)(2,1)}, bf16[75,1,128]{0,2,1:T(8,128)(2,1)}, u32[]{:S(2)}, u32[]{:S(2)}) collective-permute-start(bf16[75,1,128]{0,2,1:T(8,128)(2,1)} %get-tuple-element.88), channel_id=1, source_target_pairs={{0,4},{4,8},{8,12},{12,16},{16,20},{20,24},{24,28},{28,32},{32,36}... | collective-permute-start | bytes 57608 | tf_op jit(solution)/shard_map/ppermute | solution.py:25
  999.1 117.5 %all-to-all-start.1 = ((bf16[64,75,4,128]{3,2,1,0:T(4,128)(2,1)}), bf16[64,75,4,128]{3,2,1,0:T(4,128)(2,1)}, u32[]{:S(2)}, u32[]{:S(2)}) async-start(bf16[64,75,4,128]{3,2,1,0:T(4,128)(2,1)} %reshape.331), calls=%async_computation.1 | async-start | bytes 9830400 | tf_op jit(solution)/shard_map/all_to_all | solution.py:148
  (128 other events, 2348.4 us)
